TPU v7x, 32 devices: a whole 2x2x4 slice. The times are simulated.
32 devices in a mesh: dp: 8 (over z, x), tensor: 4 (over y, core).
Axes of the slice: x: 2, y: 2, z: 4, core: 2. Of those that a mesh axis runs over, the one named last changes fastest.
Arguments:
- patches: bfloat16 [16384, 768], P(('dp', 'tensor')), may hold values from -6 to 6
- counts: int32 [8, 3], P('dp'), may hold values from 1 to 2, as said below
- norm_gain: float32 [2, 768], replicated, may hold values from 0.5 to 1.5
- norm_bias: float32 [2, 768], replicated, may hold values from -3 to 3
- w_qkv: bfloat16 [768, 3, 768], P(None, None, 'tensor'), may hold values from -0.21875 to 0.21875
- b_qv: float32 [2, 768], P(None, 'tensor'), may hold values from -3 to 3
- w_out: bfloat16 [768, 768], P('tensor'), may hold values from -0.625 to 0.625
- out_bias: float32 [2, 768], replicated, may hold values from -3 to 3
- w_up: bfloat16 [768, 3072], P(None, 'tensor'), may hold values from -0.21875 to 0.21875
- b_up: float32 [3072], P('tensor'), may hold values from -3 to 3
- w_down: bfloat16 [3072, 768], P('tensor'), may hold values from -0.109375 to 0.109375
- cotangent: bfloat16 [16384, 768], P(('dp', 'tensor')), may hold values from -6 to 6
Outputs:
- encoded: bfloat16 [16384, 768], P(('dp', 'tensor'))
- patches_grad: bfloat16 [16384, 768], P(('dp', 'tensor'))
- norm_gain_grad: float32 [2, 768], replicated
- norm_bias_grad: float32 [2, 768], replicated
- w_qkv_grad: float32 [768, 3, 768], P('dp', None, 'tensor')
- b_qv_grad: float32 [2, 768], replicated
- w_out_grad: float32 [768, 768], P('tensor', 'dp')
- out_bias_grad: float32 [2, 768], replicated
- w_up_grad: float32 [768, 3072], P('dp', 'tensor')
- b_up_grad: float32 [3072], replicated
- w_down_grad: float32 [3072, 768], P('tensor', 'dp')
Inputs may be any that keep to these rules, and one draw needn't show every extreme that they name: `counts`: in every column some group has exactly 2 images of that size; every group has at least one image of each size.
All inputs are finite; a program needn't handle non-finite values.
Results may differ from a plain program's by a relative error of at most 0.015.
Values may be sent and summed in bfloat16 or wider, within the bound.
A program may use at most 192 MiB of HBM per device.

v0:
```python
import jax
import jax.numpy as jnp
from jax import lax
from jax.sharding import PartitionSpec as P

D = 768
HEADS = 12
HEAD_DIM = 64
FF = 3072
SIDE_S = 12
SIDE_M = 15
SIDE_L = 20
BLOCK = 512
TOK_DEV = 2048
EPSILON = 1e-06


def layout(group_counts):
    positions = jnp.arange(TOK_DEV, dtype=jnp.int32)
    area_small = SIDE_S * SIDE_S
    area_middle = SIDE_M * SIDE_M
    area_large = SIDE_L * SIDE_L
    end_small = group_counts[0] * area_small
    end_middle = end_small + group_counts[1] * area_middle
    end_large = end_middle + group_counts[2] * area_large
    size_class = (positions >= end_small).astype(jnp.int32) + (positions >= end_middle).astype(
        jnp.int32
    )
    begins = jnp.where(size_class == 0, 0, jnp.where(size_class == 1, end_small, end_middle))
    area_len = jnp.where(
        size_class == 0, area_small, jnp.where(size_class == 1, area_middle, area_large)
    )
    side_len = jnp.where(size_class == 0, SIDE_S, jnp.where(size_class == 1, SIDE_M, SIDE_L))
    within = positions - begins
    picture_index = within // area_len
    within_image = within % area_len
    is_valid = positions < end_large
    segment = jnp.where(is_valid, size_class * 16 + picture_index, 255)
    grid_row = (within_image // side_len).astype(jnp.float32)
    grid_col = (within_image % side_len).astype(jnp.float32)
    return (segment, grid_row, grid_col, is_valid.astype(jnp.float32))


def normalize(values, gain_row, shift_row):
    centred = values - jnp.mean(values, axis=-1, keepdims=True)
    spread = jnp.mean(centred * centred, axis=-1, keepdims=True)
    return centred * lax.rsqrt(spread + EPSILON) * gain_row + shift_row


def slopes_of(first_head, count_heads):
    head_number = (first_head + jnp.arange(count_heads, dtype=jnp.int32)).astype(jnp.float32) + 1.0
    return jnp.exp2(-8.0 * head_number / HEADS)


def distances(row_query, col_query, row_key, col_key):
    delta_row = row_query[:, None] - row_key[None, :]
    delta_col = col_query[:, None] - col_key[None, :]
    return jnp.sqrt(delta_row * delta_row + delta_col * delta_col)


def on_device(
    patches,
    counts,
    norm_gain,
    norm_bias,
    w_qkv,
    b_qv,
    w_out,
    out_bias,
    w_up,
    b_up,
    w_down,
    cotangent,
):
    local_rows = patches.shape[0]
    width_here = w_qkv.shape[2]
    heads_here = width_here // HEAD_DIM
    ff_here = w_up.shape[1]
    tensor_pos = lax.axis_index("tensor")
    score_scale = HEAD_DIM ** (-0.5)
    block_count = TOK_DEV // BLOCK
    segment, grid_row, grid_col, is_valid = layout(counts[0])
    keep_rows = lax.dynamic_slice_in_dim(is_valid, tensor_pos * local_rows, local_rows)[:, None]
    slopes = slopes_of(tensor_pos * heads_here, heads_here)
    inputs = patches.astype(jnp.float32)
    normed_local = normalize(inputs, norm_gain[0], norm_bias[0]).astype(jnp.bfloat16)
    normed = lax.all_gather(normed_local, "tensor", axis=0, tiled=True)
    projected = jnp.einsum("td,dsc->tsc", normed, w_qkv, preferred_element_type=jnp.float32)
    queries = (projected[:, 0] + b_qv[0]).astype(jnp.bfloat16)
    key_heads = projected[:, 1].astype(jnp.bfloat16).reshape(TOK_DEV, heads_here, HEAD_DIM)
    value_heads = (
        (projected[:, 2] + b_qv[1]).astype(jnp.bfloat16).reshape(TOK_DEV, heads_here, HEAD_DIM)
    )

    def block_scores(offset):
        query_block = lax.dynamic_slice_in_dim(queries, offset, BLOCK).reshape(
            BLOCK, heads_here, HEAD_DIM
        )
        raw_scores = (
            jnp.einsum("qhe,khe->hqk", query_block, key_heads, preferred_element_type=jnp.float32)
            * score_scale
        )
        near_dist = distances(
            lax.dynamic_slice_in_dim(grid_row, offset, BLOCK),
            lax.dynamic_slice_in_dim(grid_col, offset, BLOCK),
            grid_row,
            grid_col,
        )
        same_image = lax.dynamic_slice_in_dim(segment, offset, BLOCK)[:, None] == segment[None, :]
        return (
            query_block,
            jnp.where(
                same_image[None], raw_scores - slopes[:, None, None] * near_dist[None], -1e30
            ),
        )

    def attend_block(block_index):
        _, scores = block_scores(block_index * BLOCK)
        highest_score = jnp.max(scores, axis=-1, keepdims=True)
        exp_terms = jnp.exp(scores - highest_score)
        totals = jnp.sum(exp_terms, axis=-1, keepdims=True)
        weights = (exp_terms / totals).astype(jnp.bfloat16)
        mixed_block = jnp.einsum(
            "hqk,khe->qhe", weights, value_heads, preferred_element_type=jnp.float32
        )
        return (
            mixed_block.reshape(BLOCK, width_here).astype(jnp.bfloat16),
            highest_score[..., 0] + jnp.log(totals[..., 0]),
        )

    mixed_blocks, log_totals = lax.map(attend_block, jnp.arange(block_count, dtype=jnp.int32))
    mixed_rows = mixed_blocks.reshape(TOK_DEV, width_here)
    attended = lax.psum_scatter(
        jnp.dot(mixed_rows, w_out, preferred_element_type=jnp.float32).astype(jnp.bfloat16),
        "tensor",
        scatter_dimension=0,
        tiled=True,
    ).astype(jnp.float32)
    after_attn = inputs + keep_rows * (attended + out_bias[0])
    normed_two_local = normalize(after_attn, norm_gain[1], norm_bias[1]).astype(jnp.bfloat16)
    normed_two = lax.all_gather(normed_two_local, "tensor", axis=0, tiled=True)
    hidden_pre = jnp.dot(normed_two, w_up, preferred_element_type=jnp.float32) + b_up
    hidden = jax.nn.gelu(hidden_pre, approximate=False).astype(jnp.bfloat16)
    branch = lax.psum_scatter(
        jnp.dot(hidden, w_down, preferred_element_type=jnp.float32).astype(jnp.bfloat16),
        "tensor",
        scatter_dimension=0,
        tiled=True,
    ).astype(jnp.float32)
    result = (after_attn + keep_rows * (branch + out_bias[1])).astype(jnp.bfloat16)
    upstream = cotangent.astype(jnp.float32)
    down_bias_grad = jnp.sum(keep_rows * upstream, axis=0)
    branch_grad = lax.all_gather(
        (keep_rows * upstream).astype(jnp.bfloat16), "tensor", axis=0, tiled=True
    )
    w_down_grad = jnp.einsum("tf,td->fd", hidden, branch_grad, preferred_element_type=jnp.float32)
    hidden_grad = jnp.einsum("td,fd->tf", branch_grad, w_down, preferred_element_type=jnp.float32)
    _, gelu_back = jax.vjp(lambda pre_act: jax.nn.gelu(pre_act, approximate=False), hidden_pre)
    pre_grad = gelu_back(hidden_grad)[0].astype(jnp.bfloat16)
    up_bias_grad = jnp.sum(pre_grad, axis=0, dtype=jnp.float32)
    w_up_grad = jnp.einsum("td,tf->df", normed_two, pre_grad, preferred_element_type=jnp.float32)
    normed_two_grad = lax.psum_scatter(
        jnp.einsum("tf,df->td", pre_grad, w_up, preferred_element_type=jnp.float32).astype(
            jnp.bfloat16
        ),
        "tensor",
        scatter_dimension=0,
        tiled=True,
    ).astype(jnp.float32)
    _, norm_two_back = jax.vjp(normalize, after_attn, norm_gain[1], norm_bias[1])
    through_two, gain_two_grad, shift_two_grad = norm_two_back(normed_two_grad)
    after_grad = upstream + through_two
    attn_bias_grad = jnp.sum(keep_rows * after_grad, axis=0)
    attn_local = (keep_rows * after_grad).astype(jnp.bfloat16)
    attn_grad = lax.all_gather(attn_local, "tensor", axis=0, tiled=True)
    w_out_grad = jnp.einsum("tc,td->cd", mixed_rows, attn_grad, preferred_element_type=jnp.float32)
    mixed_grad = jnp.einsum(
        "td,cd->tc", attn_grad, w_out, preferred_element_type=jnp.float32
    ).astype(jnp.bfloat16)
    mixed_heads = mixed_grad.reshape(TOK_DEV, heads_here, HEAD_DIM)

    def back_block(running, block_index):
        key_acc, value_acc = running
        offset = block_index * BLOCK
        query_block, scores = block_scores(offset)
        weights = jnp.exp(
            scores - lax.dynamic_index_in_dim(log_totals, block_index, keepdims=False)[..., None]
        )
        grad_block = lax.dynamic_slice_in_dim(mixed_heads, offset, BLOCK)
        value_acc = value_acc + jnp.einsum(
            "hqk,qhe->khe",
            weights.astype(jnp.bfloat16),
            grad_block,
            preferred_element_type=jnp.float32,
        )
        weight_grad = jnp.einsum(
            "qhe,khe->hqk", grad_block, value_heads, preferred_element_type=jnp.float32
        )
        score_grad = (
            weights * (weight_grad - jnp.sum(weights * weight_grad, axis=-1, keepdims=True))
        ).astype(jnp.bfloat16)
        query_grad_block = (
            jnp.einsum("hqk,khe->qhe", score_grad, key_heads, preferred_element_type=jnp.float32)
            * score_scale
        )
        key_acc = (
            key_acc
            + jnp.einsum(
                "hqk,qhe->khe", score_grad, query_block, preferred_element_type=jnp.float32
            )
            * score_scale
        )
        return (
            (key_acc, value_acc),
            query_grad_block.reshape(BLOCK, width_here).astype(jnp.bfloat16),
        )

    zero_heads = jnp.zeros((TOK_DEV, heads_here, HEAD_DIM), jnp.float32)
    (key_acc, value_acc), query_blocks = lax.scan(
        back_block, (zero_heads, zero_heads), jnp.arange(block_count, dtype=jnp.int32)
    )
    query_grad = query_blocks.reshape(TOK_DEV, width_here)
    key_grad = key_acc.reshape(TOK_DEV, width_here).astype(jnp.bfloat16)
    value_grad = value_acc.reshape(TOK_DEV, width_here).astype(jnp.bfloat16)
    projected_grad = jnp.stack([query_grad, key_grad, value_grad], axis=1)
    qv_bias_grad = jnp.stack(
        [
            jnp.sum(query_grad, axis=0, dtype=jnp.float32),
            jnp.sum(value_grad, axis=0, dtype=jnp.float32),
        ]
    )
    w_qkv_grad = jnp.einsum(
        "td,tsc->dsc", normed, projected_grad, preferred_element_type=jnp.float32
    )
    normed_grad = lax.psum_scatter(
        jnp.einsum("tsc,dsc->td", projected_grad, w_qkv, preferred_element_type=jnp.float32).astype(
            jnp.bfloat16
        ),
        "tensor",
        scatter_dimension=0,
        tiled=True,
    ).astype(jnp.float32)
    qv_full = lax.dynamic_update_slice_in_dim(
        jnp.zeros((2, D), jnp.float32), qv_bias_grad, tensor_pos * width_here, 1
    )
    _, norm_one_back = jax.vjp(normalize, inputs, norm_gain[0], norm_bias[0])
    through_one, gain_one_grad, shift_one_grad = norm_one_back(normed_grad)
    input_grad = (after_grad + through_one).astype(jnp.bfloat16)
    up_full = lax.dynamic_update_slice_in_dim(
        jnp.zeros((FF,), jnp.float32), up_bias_grad, tensor_pos * ff_here, 0
    )
    gains_grad, shifts_grad, outer_grad, qv_sum, up_sum = lax.psum(
        (
            jnp.stack([gain_one_grad, gain_two_grad]),
            jnp.stack([shift_one_grad, shift_two_grad]),
            jnp.stack([attn_bias_grad, down_bias_grad]),
            qv_full,
            up_full,
        ),
        ("dp", "tensor"),
    )
    qkv_part, out_part, up_part, down_part = (
        lax.psum_scatter(w_qkv_grad, "dp", scatter_dimension=0, tiled=True),
        lax.psum_scatter(w_out_grad, "dp", scatter_dimension=1, tiled=True),
        lax.psum_scatter(w_up_grad, "dp", scatter_dimension=0, tiled=True),
        lax.psum_scatter(w_down_grad, "dp", scatter_dimension=1, tiled=True),
    )
    return (
        result,
        input_grad,
        gains_grad,
        shifts_grad,
        qkv_part,
        qv_sum,
        out_part,
        outer_grad,
        up_part,
        up_sum,
        down_part,
    )


def solution(mesh):
    placed = (
        P(("dp", "tensor"), None),
        P("dp", None),
        P(),
        P(),
        P(None, None, "tensor"),
        P(None, "tensor"),
        P("tensor", None),
        P(),
        P(None, "tensor"),
        P("tensor"),
        P("tensor", None),
        P(("dp", "tensor"), None),
    )
    return jax.shard_map(
        on_device,
        mesh=mesh,
        in_specs=placed,
        out_specs=(
            P(("dp", "tensor"), None),
            P(("dp", "tensor"), None),
            P(),
            P(),
            P("dp", None, "tensor"),
            P(),
            P("tensor", "dp"),
            P(),
            P("dp", "tensor"),
            P(),
            P("tensor", "dp"),
        ),
        check_vma=False,
    )
```

profile of v0, /device:TPU:0, one launch (start us, length us, event | category | flops | bytes accessed | tf_op | source)
XLA Modules:
  0.0 811.1 jit_solution(15307755754679857029)
XLA Ops:
  19.1 26.9 %all-gather.5.cloned.1.call-done = bf16[2048,768]{1,0:T(8,128)(2,1)} async-done(((bf16[512,768]{1,0:T(8,128)(2,1)}), bf16[2048,768]{1,0:T(8,128)(2,1)}) %all-gather.5.cloned.1.call-update) | async-done | bytes 3145744 | tf_op jit(solution)/shard_map/all_gather | solution.py:87
  46.0 3.9 fusion.73
  52.4 80.2 %while.28 = (s32[]{:T(128)}, bf16[4,512,192]{1,2,0:T(8,128)(2,1)}, f32[4,3,512]{2,1,0:T(4,128)}, s32[4]{0:T(128)}, s32[2048]{0:T(1024)S(1)}, /*index=5*/bf16[204...) while((s32[]{:T(128)}, bf16[4,512,192]{1,2,0:T(8,128)(2,1)}, ...), condition=%wide.region_5.6_spmd.clone, body=%wide.region_2.5_spmd.clone.sunk | while | flops 868317696 | bytes 61567260 | solution.py:131
  62.1 4.5 fusion.132
  66.5 4.7 fusion.133
  78.5 3.6 fusion.131
  82.1 4.5 fusion.132
  86.5 4.7 fusion.133
  102.0 4.5 fusion.132
  106.5 4.7 fusion.133
  122.0 4.5 fusion.132
  126.5 4.7 fusion.133
  135.2 3.7 convolution_convert_fusion.2
  140.7 36.2 %reduce-scatter.11.cloned.1.call-done = bf16[512,768]{1,0:T(8,128)(2,1)} async-done(((bf16[2048,768]{1,0:T(8,128)(2,1)}), bf16[512,768]{1,0:T(8,128)(2,1)}) %reduce-scatter.11.cloned.1.call-update) | async-done | bytes 786448 | tf_op jit(solution)/shard_map/reduce_scatter | solution.py:133
  184.6 28.0 %all-gather.7.cloned.1.call-done = bf16[2048,768]{1,0:T(8,128)(2,1)} async-done(((bf16[512,768]{1,0:T(8,128)(2,1)}), bf16[2048,768]{1,0:T(8,128)(2,1)}) %all-gather.7.cloned.1.call-update) | async-done | bytes 3145744 | tf_op jit(solution)/shard_map/all_gather | solution.py:141
  212.6 7.5 fusion.74
  220.1 23.0 %all-gather.9.cloned.1.call-done = bf16[2048,768]{1,0:T(8,128)(2,1)} async-done(((bf16[512,768]{1,0:T(8,128)(2,1)}), bf16[2048,768]{1,0:T(8,128)(2,1)}) %all-gather.9.cloned.1.call-update) | async-done | bytes 3145744 | tf_op jit(solution)/shard_map/all_gather | solution.py:153
  243.2 20.2 %convert_reduce_fusion = (f32[768]{0:T(1024)}, bf16[2048,768]{1,0:T(8,128)(2,1)S(1)}, f32[2048,768]{1,0:T(8,128)}) fusion(f32[2048,768]{1,0:T(8,128)} %fusion.74, f32[768]{0:T(1024)} %param.25, bf16[2048,768]{1,0:T(8,128)(2,1)} %all-gather.9.cloned.1.call-done, bf16[768,768]{1,0:T(8,128)(2,1)S(1)} %copy-done), kind=kOutput, calls=%fused_computation.43 | convolution fusion | flops 2533883136 | bytes 20060160 | tf_op jit(solution)/shard_map/td,fd->tf/dot_general | solution.py:157
  265.0 4.0 convolution_convert_fusion
  269.1 5.5 multiply_convert_fusion.1
  276.3 4.0 convolution_convert_fusion.1
  280.6 26.5 %reduce-scatter.15.cloned.1.call-done = bf16[512,768]{1,0:T(8,128)(2,1)} async-done(((bf16[2048,768]{1,0:T(8,128)(2,1)}), bf16[512,768]{1,0:T(8,128)(2,1)}) %reduce-scatter.15.cloned.1.call-update) | async-done | bytes 786448 | tf_op jit(solution)/shard_map/reduce_scatter | solution.py:162
  309.8 37.6 %reduce-scatter.13.cloned.1.call-done = bf16[512,768]{1,0:T(8,128)(2,1)} async-done(((bf16[2048,768]{1,0:T(8,128)(2,1)}), bf16[512,768]{1,0:T(8,128)(2,1)}) %reduce-scatter.13.cloned.1.call-update) | async-done | bytes 786448 | tf_op jit(solution)/shard_map/reduce_scatter | solution.py:144
  354.0 28.6 %all-gather.11.cloned.1.call-done = bf16[2048,768]{1,0:T(8,128)(2,1)} async-done(((bf16[512,768]{1,0:T(8,128)(2,1)}), bf16[2048,768]{1,0:T(8,128)(2,1)}) %all-gather.11.cloned.1.call-update) | async-done | bytes 3145744 | tf_op jit(solution)/shard_map/all_gather | solution.py:175
  382.6 4.1 convolution_bitcast_fusion
  386.8 4.0 convolution_convert_fusion.3
  391.7 141.8 %while.29 = (s32[]{:T(128)}, f32[2048,3,64]{0,2,1:T(8,128)}, f32[2048,3,64]{0,2,1:T(8,128)}, bf16[4,512,192]{1,2,0:T(8,128)(2,1)}, s32[4]{0:T(128)S(1)}, /*index...) while((s32[]{:T(128)}, f32[2048,3,64]{0,2,1:T(8,128)}, ...), condition=%wide.region_15.16_spmd.clone, body=%wide.region_13.15_spmd.clone.sunk | while | flops 2056321536 | bytes 143663600 | solution.py:219
  401.9 8.7 %multiply_reduce_fusion.4 = (f32[3,512]{1,0:T(4,128)S(1)}, f32[3,512,2048]{2,1,0:T(8,128)}) fusion(f32[3,512,2048]{2,1,0:T(8,128)S(1)} %fusion.144, f32[3,512]{1,0:T(4,128)S(1)} %dynamic-slice_bitcast_fusion.2, f32[512,2048]{1,0:T(8,128)S(1)} %add_sqrt_fusion.5, f32[3]{0:T(128)S(1)} %multiply_exponential_fusion.5, ...), kind=kOutput, calls=%fused_computation.18.clone.1 | convolution fusion | flops 424671744 | bytes 31404044 | tf_op jit(solution)/shard_map/while/body/eval_jaxpr/qhe,khe->hqk/dot_general | solution.py:100
  410.6 5.6 multiply_convert_fusion.4
  416.3 6.2 fusion.146
  437.4 8.7 %multiply_reduce_fusion.4 = (f32[3,512]{1,0:T(4,128)S(1)}, f32[3,512,2048]{2,1,0:T(8,128)}) fusion(f32[3,512,2048]{2,1,0:T(8,128)S(1)} %fusion.144, f32[3,512]{1,0:T(4,128)S(1)} %dynamic-slice_bitcast_fusion.2, f32[512,2048]{1,0:T(8,128)S(1)} %add_sqrt_fusion.5, f32[3]{0:T(128)S(1)} %multiply_exponential_fusion.5, ...), kind=kOutput, calls=%fused_computation.18.clone.1 | convolution fusion | flops 424671744 | bytes 31404044 | tf_op jit(solution)/shard_map/while/body/eval_jaxpr/qhe,khe->hqk/dot_general | solution.py:100
  446.1 5.6 multiply_convert_fusion.4
  451.7 6.1 fusion.146
  472.8 8.7 %multiply_reduce_fusion.4 = (f32[3,512]{1,0:T(4,128)S(1)}, f32[3,512,2048]{2,1,0:T(8,128)}) fusion(f32[3,512,2048]{2,1,0:T(8,128)S(1)} %fusion.144, f32[3,512]{1,0:T(4,128)S(1)} %dynamic-slice_bitcast_fusion.2, f32[512,2048]{1,0:T(8,128)S(1)} %add_sqrt_fusion.5, f32[3]{0:T(128)S(1)} %multiply_exponential_fusion.5, ...), kind=kOutput, calls=%fused_computation.18.clone.1 | convolution fusion | flops 424671744 | bytes 31404044 | tf_op jit(solution)/shard_map/while/body/eval_jaxpr/qhe,khe->hqk/dot_general | solution.py:100
  481.5 5.6 multiply_convert_fusion.4
  487.1 6.1 fusion.146
  508.2 8.7 %multiply_reduce_fusion.4 = (f32[3,512]{1,0:T(4,128)S(1)}, f32[3,512,2048]{2,1,0:T(8,128)}) fusion(f32[3,512,2048]{2,1,0:T(8,128)S(1)} %fusion.144, f32[3,512]{1,0:T(4,128)S(1)} %dynamic-slice_bitcast_fusion.2, f32[512,2048]{1,0:T(8,128)S(1)} %add_sqrt_fusion.5, f32[3]{0:T(128)S(1)} %multiply_exponential_fusion.5, ...), kind=kOutput, calls=%fused_computation.18.clone.1 | convolution fusion | flops 424671744 | bytes 31404044 | tf_op jit(solution)/shard_map/while/body/eval_jaxpr/qhe,khe->hqk/dot_general | solution.py:100
  516.9 5.6 multiply_convert_fusion.4
  522.5 6.1 fusion.146
  540.0 5.7 bitcast_convert_fusion
  545.8 7.0 fusion.76
  552.9 7.8 fusion.75
  561.0 6.0 fusion.32
  576.5 7.3 reduce-scatter.17.cloned.1.call-done
  590.2 41.6 %all-reduce = (f32[2,768]{1,0:T(2,128)}, f32[2,768]{1,0:T(2,128)}, f32[2,768]{1,0:T(2,128)}, f32[2,768]{1,0:T(2,128)}, f32[3072]{0:T(1024)}) all-reduce(f32[2,768]{1,0:T(2,128)} %pad_maximum_fusion.3, f32[2,768]{1,0:T(2,128)} %pad_maximum_fusion.4, ...), channel_id=1, replica_groups=mesh['dp'=8,'tensor'=4] {'dp','tensor'}, use_global_device_ids=true, to_apply=%region_21.22 | all-reduce | flops 9216 | bytes 73728 | tf_op jit(solution)/shard_map/psum | solution.py:252
  635.5 22.4 %reduce-scatter.23.cloned.1.call-done = f32[768,96]{0,1:T(8,128)} async-done(((f32[768,768]{0,1:T(8,128)}), f32[768,96]{0,1:T(8,128)}) %reduce-scatter.23.cloned.1.call-update) | async-done | bytes 294928 | tf_op jit(solution)/shard_map/reduce_scatter | solution.py:266
  658.0 72.9 %reduce-scatter.21.cloned.1.call-done = f32[96,768]{1,0:T(8,128)} async-done(((f32[768,768]{1,0:T(8,128)}), f32[96,768]{1,0:T(8,128)}) %reduce-scatter.21.cloned.1.call-update) | async-done | bytes 294928 | tf_op jit(solution)/shard_map/reduce_scatter | solution.py:265
  730.9 72.9 %reduce-scatter.19.cloned.1.call-done = f32[96,3,192]{2,0,1:T(8,128)} async-done(((f32[768,3,192]{2,0,1:T(8,128)}), f32[96,3,192]{2,0,1:T(8,128)}) %reduce-scatter.19.cloned.1.call-update) | async-done | bytes 221200 | tf_op jit(solution)/shard_map/reduce_scatter | solution.py:263
  (324 shorter events, 150.5 us)
Async XLA Ops:
  7.2 236.0 %copy-start = (bf16[768,768]{1,0:T(8,128)(2,1)S(1)}, bf16[768,768]{1,0:T(8,128)(2,1)}, u32[]{:S(2)}) copy-start(bf16[768,768]{1,0:T(8,128)(2,1)} %param.26) | copy-start | bytes 3538948
  7.2 7.5 copy-start.52
  7.2 8.2 %copy-start.51 = (s32[1,3]{1,0:T(1,128)S(1)}, s32[1,3]{1,0:T(1,128)}, u32[]{:S(2)}) copy-start(s32[1,3]{1,0:T(1,128)} %param.17) | copy-start | bytes 40
  7.2 38.8 %copy-start.54 = (bf16[768,3,192]{0,2,1:T(8,128)(2,1)S(1)}, bf16[768,3,192]{0,2,1:T(8,128)(2,1)}, u32[]{:S(2)}) copy-start(bf16[768,3,192]{0,2,1:T(8,128)(2,1)} %param.20) | copy-start | bytes 2654212
  7.2 38.8 %all-gather.5.cloned.1.call-start = ((), (), s32[]{:S(2)}) async-start(), calls=%async_computation.8 | async-start | bytes 3932160 | tf_op jit(solution)/shard_map/all_gather | solution.py:87
  8.7 41.2 %copy-start.31 = (f32[512]{0:T(512)}, f32[512]{0:T(512)S(1)}, u32[]{:S(2)}) copy-start(f32[512]{0:T(512)S(1)} %broadcast_multiply_fusion.1) | copy-start | bytes 6148
  10.8 39.1 %copy-start.37 = (f32[512]{0:T(512)}, f32[512]{0:T(512)S(1)}, u32[]{:S(2)}) copy-start(f32[512]{0:T(512)S(1)} %fusion.65) | copy-start | bytes 6148
  12.2 37.7 %copy-start.27 = (f32[768]{0:T(1024)}, f32[768]{0:T(1024)S(1)}, u32[]{:S(2)}) copy-start(f32[768]{0:T(1024)S(1)} %get-tuple-element.314) | copy-start | bytes 9220
  14.6 162.3 %reduce-scatter.11.cloned.1.call-start = ((), (), s32[]{:S(2)}) async-start(), calls=%async_computation.9 | async-start | bytes 3932160 | tf_op jit(solution)/shard_map/reduce_scatter | solution.py:133
  132.5 6.4 copy-start.14
  138.9 38.1 %copy-start.2 = (bf16[512,768]{1,0:T(8,128)(2,1)S(1)}, bf16[512,768]{1,0:T(8,128)(2,1)}, u32[]{:S(2)}) copy-start(bf16[512,768]{1,0:T(8,128)(2,1)} %param.16) | copy-start | bytes 2359300
  138.9 73.7 %all-gather.7.cloned.1.call-start = ((), (), s32[]{:S(2)}) async-start(), calls=%async_computation.10 | async-start | bytes 3932160 | tf_op jit(solution)/shard_map/all_gather | solution.py:141
  184.0 59.2 %all-gather.9.cloned.1.call-start = ((), (), s32[]{:S(2)}) async-start(), calls=%async_computation.12 | async-start | bytes 3932160 | tf_op jit(solution)/shard_map/all_gather | solution.py:153
  184.5 122.5 %reduce-scatter.15.cloned.1.call-start = ((), (), s32[]{:S(2)}) async-start(), calls=%async_computation.13 | async-start | bytes 3932160 | tf_op jit(solution)/shard_map/reduce_scatter | solution.py:162
  243.2 21.8 %copy-start.53 = (bf16[768,768]{1,0:T(8,128)(2,1)S(1)}, bf16[768,768]{1,0:T(8,128)(2,1)}, u32[]{:S(2)}) copy-start(bf16[768,768]{1,0:T(8,128)(2,1)} %param.24) | copy-start | bytes 3538948
  269.0 78.3 %reduce-scatter.13.cloned.1.call-start = ((), (), s32[]{:S(2)}) async-start(), calls=%async_computation.11 | async-start | bytes 3932160 | tf_op jit(solution)/shard_map/reduce_scatter | solution.py:144
  280.3 26.8 %copy-start.26 = (f32[768]{0:T(1024)S(1)}, f32[768]{0:T(1024)}, u32[]{:S(2)}) copy-start(f32[768]{0:T(1024)} %get-tuple-element.231) | copy-start | bytes 9220
  280.3 26.8 %copy-start.30 = (f32[512]{0:T(512)S(1)}, f32[512]{0:T(512)}, u32[]{:S(2)}) copy-start(f32[512]{0:T(512)} %dynamic-slice_convert_fusion) | copy-start | bytes 6148
  280.3 26.8 %copy-start.33 = (f32[768]{0:T(1024)S(1)}, f32[768]{0:T(1024)}, u32[]{:S(2)}) copy-start(f32[768]{0:T(1024)} %get-tuple-element.313) | copy-start | bytes 9220
  280.3 26.8 %copy-start.35 = (f32[512]{0:T(512)S(1)}, f32[512]{0:T(512)}, u32[]{:S(2)}) copy-start(f32[512]{0:T(512)} %copy-done.34) | copy-start | bytes 6148
  280.3 26.8 %copy-start.40 = (f32[512]{0:T(512)S(1)}, f32[512]{0:T(512)}, u32[]{:S(2)}) copy-start(f32[512]{0:T(512)} %copy-done.39) | copy-start | bytes 6148
  280.3 29.5 %copy-start.44 = (f32[512]{0:T(512)S(1)}, f32[512]{0:T(512)}, u32[]{:S(2)}) copy-start(f32[512]{0:T(512)} %copy-done.43) | copy-start | bytes 6148
  280.3 67.0 %copy-start.46 = (f32[768]{0:T(1024)S(1)}, f32[768]{0:T(1024)}, u32[]{:S(2)}) copy-start(f32[768]{0:T(1024)} %get-tuple-element.230) | copy-start | bytes 9220
  280.4 102.2 %all-gather.11.cloned.1.call-start = ((), (), s32[]{:S(2)}) async-start(), calls=%async_computation.14 | async-start | bytes 3932160 | tf_op jit(solution)/shard_map/all_gather | solution.py:175
  309.8 42.1 %copy-start.15 = (bf16[512,768]{1,0:T(8,128)(2,1)S(1)}, bf16[512,768]{1,0:T(8,128)(2,1)}, u32[]{:S(2)}) copy-start(bf16[512,768]{1,0:T(8,128)(2,1)} %param.27) | copy-start | bytes 2359300
  350.7 31.9 %copy-start.18 = (bf16[4,24,8,512]{3,2,0,1:T(8,128)(2,1)S(1)}, bf16[4,24,8,512]{3,2,0,1:T(8,128)(2,1)}, u32[]{:S(2)}) copy-start(bf16[4,24,8,512]{3,2,0,1:T(8,128)(2,1)} %copy-done.17) | copy-start | bytes 2359300
  350.7 36.0 %copy-start.41 = (f32[512]{0:T(512)}, f32[512]{0:T(512)S(1)}, u32[]{:S(2)}) copy-start(f32[512]{0:T(512)S(1)} %negate_multiply_fusion.2) | copy-start | bytes 6148
  353.9 221.0 %reduce-scatter.25.cloned.1.call-start = ((), (), s32[]{:S(2)}) async-start(), calls=%async_computation.19 | async-start | bytes 884736
  354.0 32.8 %copy-start.24 = (bf16[192,768]{1,0:T(8,128)(2,1)S(1)}, bf16[192,768]{1,0:T(8,128)(2,1)}, u32[]{:S(2)}) copy-start(bf16[192,768]{1,0:T(8,128)(2,1)} %param.22) | copy-start | bytes 884740
  386.7 197.1 %reduce-scatter.17.cloned.1.call-start = ((), (), s32[]{:S(2)}) async-start(), calls=%async_computation.15 | async-start | bytes 3932160 | tf_op jit(solution)/shard_map/reduce_scatter | solution.py:235
  410.6 5.6 copy-start.6
  446.1 5.6 copy-start.6
  481.5 5.6 copy-start.6
  516.9 5.6 copy-start.6
  545.8 112.2 %reduce-scatter.23.cloned.1.call-start = ((), (), s32[]{:S(2)}) async-start(), calls=%async_computation.18 | async-start | bytes 2654208 | tf_op jit(solution)/shard_map/reduce_scatter | solution.py:266
  552.8 8.2 %copy-start.21 = (bf16[2048,3,64]{0,2,1:T(8,128)(2,1)S(1)}, bf16[2048,3,64]{0,2,1:T(8,128)(2,1)}, u32[]{:S(2)}) copy-start(bf16[2048,3,64]{0,2,1:T(8,128)(2,1)} %convert_element_type.191) | copy-start | bytes 2359300
  552.8 8.2 %copy-start.23 = (bf16[2048,3,64]{0,2,1:T(8,128)(2,1)S(1)}, bf16[2048,3,64]{0,2,1:T(8,128)(2,1)}, u32[]{:S(2)}) copy-start(bf16[2048,3,64]{0,2,1:T(8,128)(2,1)} %copy-done.22) | copy-start | bytes 2359300
  552.8 178.1 %reduce-scatter.21.cloned.1.call-start = ((), (), s32[]{:S(2)}) async-start(), calls=%async_computation.17 | async-start | bytes 2654208 | tf_op jit(solution)/shard_map/reduce_scatter | solution.py:265
  560.7 8.7 %copy-start.45 = (f32[768]{0:T(1024)S(1)}, f32[768]{0:T(1024)}, u32[]{:S(2)}) copy-start(f32[768]{0:T(1024)} %get-tuple-element.229) | copy-start | bytes 9220
  560.7 12.1 %copy-start.16 = (bf16[4,512,192]{1,2,0:T(8,128)(2,1)S(1)}, bf16[4,512,192]{1,2,0:T(8,128)(2,1)}, u32[]{:S(2)}) copy-start(bf16[4,512,192]{1,2,0:T(8,128)(2,1)} %get-tuple-element.145) | copy-start | bytes 2359300
  560.7 243.1 %reduce-scatter.19.cloned.1.call-start = ((), (), s32[]{:S(2)}) async-start(), calls=%async_computation.16 | async-start | bytes 2654208 | tf_op jit(solution)/shard_map/reduce_scatter | solution.py:263
  567.1 16.7 %copy-start.3 = (bf16[512,768]{1,0:T(8,128)(2,1)S(1)}, bf16[512,768]{1,0:T(8,128)(2,1)}, u32[]{:S(2)}) copy-start(bf16[512,768]{1,0:T(8,128)(2,1)} %param.16) | copy-start | bytes 2359300
  567.1 16.7 %copy-start.28 = (f32[768]{0:T(1024)S(1)}, f32[768]{0:T(1024)}, u32[]{:S(2)}) copy-start(f32[768]{0:T(1024)} %copy-done.27) | copy-start | bytes 9220
  567.1 16.7 %copy-start.32 = (f32[512]{0:T(512)S(1)}, f32[512]{0:T(512)}, u32[]{:S(2)}) copy-start(f32[512]{0:T(512)} %copy-done.31) | copy-start | bytes 6148
  567.1 19.2 %copy-start.38 = (f32[512]{0:T(512)S(1)}, f32[512]{0:T(512)}, u32[]{:S(2)}) copy-start(f32[512]{0:T(512)} %copy-done.37) | copy-start | bytes 6148
  567.1 65.5 %copy-start.13 = (f32[512,768]{1,0:T(8,128)S(1)}, f32[512,768]{1,0:T(8,128)}, u32[]{:S(2)}) copy-start(f32[512,768]{1,0:T(8,128)} %copy-done.12) | copy-start | bytes 4718596
  583.8 5.8 copy-start.47
  585.5 218.3 %copy-start.1 = (bf16[768,768]{1,0:T(8,128)(2,1)S(1)}, bf16[768,768]{1,0:T(8,128)(2,1)}, u32[]{:S(2)}) copy-start(bf16[768,768]{1,0:T(8,128)(2,1)} %param.26) | copy-start | bytes 3538948
  (35 other events, 89.8 us)
Sparse Core Ops, SparseCore 0:
  14.8 31.2 all-gather.4
  139.1 37.8 reduce-scatter.10
  184.1 28.4 all-gather.6
  214.6 28.4 all-gather.8
  269.1 37.8 reduce-scatter.14
  309.5 37.8 reduce-scatter.12
  354.0 28.4 all-gather.10
  386.8 63.2 reduce-scatter.24
  545.9 37.8 reduce-scatter.16
  587.7 70.1 reduce-scatter.22
  662.0 68.8 reduce-scatter.20
  734.8 68.9 reduce-scatter.18
where the time goes:
time: 816 us; the launch traced here: 811 us
  waiting for transfers between devices  383 us (47%)
  matrix products  195 us (24%)
  other arithmetic  106 us (13%)
  local copies, waits for them, and re-layouts  52.8 us (6%)
  blocking collectives  41.6 us (5%)
  between operations  17.1 us (2%)
  loops' own time  14 us (2%)
    reduce_scatter x1, waiting for transfers between devices, on_device(): lax.psum_scatter(w_up_grad, 'dp', scatter_dimension=0, tiled=True)  72.9 us
    reduce_scatter x1, waiting for transfers between devices, on_device(): lax.psum_scatter(w_qkv_grad, 'dp', scatter_dimension=0, tiled=True)  72.9 us
    dot_general x8, matrix products, block_scores(): jnp.einsum('qhe,khe->hqk', query_block, key_heads, preferred_element_type...  49.1 us
    psum x1, blocking collectives, on_device(): lax.psum((jnp.stack([gain_one_grad, gain_two_grad]), jnp.stack([shift_one...  41.6 us
    reduce_scatter x1, waiting for transfers between devices, on_device(): lax.psum_scatter(jnp.dot(hidden, w_down, preferred_element_type=jnp.float...  37.6 us
    reduce_scatter x1, waiting for transfers between devices, on_device(): lax.psum_scatter(jnp.dot(mixed_rows, w_out, preferred_element_type=jnp.fl...  36.2 us
    all_gather x1, waiting for transfers between devices, on_device(): attn_grad = lax.all_gather(attn_local, 'tensor', axis=0, tiled=True)  28.6 us
    all_gather x1, waiting for transfers between devices, on_device(): normed_two = lax.all_gather(normed_two_local, 'tensor', axis=0, tiled=True)  28 us
  transfers between devices with their start and end apart: 12, of which 11 were waited for; matrix products, arithmetic and copies ran while one was open for 26% of the time, Pallas kernels for 0%

commit v1 on v0

--- a/solution.py
+++ b/solution.py
@@ -13,6 +13,28 @@
 BLOCK = 512
 TOK_DEV = 2048
 EPSILON = 1e-06
+
+
+def joined_along(pieces, dim):
+    dims = list(pieces.shape[1:])
+    dims[dim] *= pieces.shape[0]
+    return jnp.moveaxis(pieces, 0, dim).reshape(dims)
+
+
+def ring_gather(x, axis, dim):
+    size = lax.axis_size(axis)
+    pairs = [(i, (i + 1) % size) for i in range(size)]
+    back = [(b, a) for a, b in pairs]
+    lower, upper = ([], [])
+    for step in range(size - 1):
+        if step % 2 == 0:
+            lower.append(lax.ppermute(lower[-1] if lower else x, axis, pairs))
+        else:
+            upper.append(lax.ppermute(upper[-1] if upper else x, axis, back))
+    pieces = jnp.stack([*lower[::-1], x, *upper])
+    shift = lax.axis_index(axis) - len(lower)
+    pieces = pieces[(jnp.arange(size) - shift) % size]
+    return joined_along(pieces, dim)
 
 
 def layout(group_counts):
@@ -172,7 +194,7 @@
     after_grad = upstream + through_two
     attn_bias_grad = jnp.sum(keep_rows * after_grad, axis=0)
     attn_local = (keep_rows * after_grad).astype(jnp.bfloat16)
-    attn_grad = lax.all_gather(attn_local, "tensor", axis=0, tiled=True)
+    attn_grad = ring_gather(attn_local, "tensor", 0)
     w_out_grad = jnp.einsum("tc,td->cd", mixed_rows, attn_grad, preferred_element_type=jnp.float32)
     mixed_grad = jnp.einsum(
         "td,cd->tc", attn_grad, w_out, preferred_element_type=jnp.float32

time: 816 us -> 822 us (level)
    ppermute x0 -> x3, waiting for transfers between devices: none -> 28.9 us  [the longest x2 28.9 us: ring_gather(): lower.append(lax.ppermute(lower[-1] if lower else x, axis, pairs))]
    all_gather x1 -> x0, waiting for transfers between devices: 28.6 us -> none  [on_device(): attn_grad = lax.all_gather(attn_local, 'tensor', axis=0, tiled=True)]
  transfers between devices with their start and end apart: 12 -> 14, of which waited for: 11 -> 12; matrix products, arithmetic and copies ran while one was open for 26% -> 26% of each run, Pallas kernels for 0% -> 0%
where the time goes in v1:
time: 822 us; the launch traced here: 817 us
  waiting for transfers between devices  382 us (46%)
  matrix products  195 us (24%)
  other arithmetic  108 us (13%)
  local copies, waits for them, and re-layouts  56.2 us (7%)
  blocking collectives  41.8 us (5%)
  between operations  16.8 us (2%)
  loops' own time  14 us (2%)
    reduce_scatter x1, waiting for transfers between devices, on_device(): lax.psum_scatter(w_qkv_grad, 'dp', scatter_dimension=0, tiled=True)  72.9 us
    reduce_scatter x1, waiting for transfers between devices, on_device(): lax.psum_scatter(w_up_grad, 'dp', scatter_dimension=0, tiled=True)  72.7 us
    dot_general x8, matrix products, block_scores(): jnp.einsum('qhe,khe->hqk', query_block, key_heads, preferred_element_type...  49.1 us
    psum x1, blocking collectives, on_device(): lax.psum((jnp.stack([gain_one_grad, gain_two_grad]), jnp.stack([shift_one...  41.8 us
    reduce_scatter x1, waiting for transfers between devices, on_device(): lax.psum_scatter(jnp.dot(hidden, w_down, preferred_element_type=jnp.float...  37.6 us
    reduce_scatter x1, waiting for transfers between devices, on_device(): lax.psum_scatter(jnp.dot(mixed_rows, w_out, preferred_element_type=jnp.fl...  36.2 us
    ppermute x2, waiting for transfers between devices, ring_gather(): lower.append(lax.ppermute(lower[-1] if lower else x, axis, pairs))  28.9 us
    all_gather x1, waiting for transfers between devices, on_device(): normed_two = lax.all_gather(normed_two_local, 'tensor', axis=0, tiled=True)  28 us
  transfers between devices with their start and end apart: 14, of which 12 were waited for; matrix products, arithmetic and copies ran while one was open for 26% of the time, Pallas kernels for 0%

profile of v1, /device:TPU:0, one launch (start us, length us, event | category | flops | bytes accessed | tf_op | source)
XLA Modules:
  0.0 817.1 jit_solution(8024319856887951667)
XLA Ops:
  19.1 26.9 %all-gather.4.cloned.1.call-done = bf16[2048,768]{1,0:T(8,128)(2,1)} async-done(((bf16[512,768]{1,0:T(8,128)(2,1)}), bf16[2048,768]{1,0:T(8,128)(2,1)}) %all-gather.4.cloned.1.call-update) | async-done | bytes 3145744 | tf_op jit(solution)/shard_map/all_gather | solution.py:109
  46.0 3.9 fusion.75
  52.4 80.2 %while.28 = (s32[]{:T(128)}, bf16[4,512,192]{1,2,0:T(8,128)(2,1)}, f32[4,3,512]{2,1,0:T(4,128)}, s32[4]{0:T(128)}, s32[2048]{0:T(1024)S(1)}, /*index=5*/bf16[204...) while((s32[]{:T(128)}, bf16[4,512,192]{1,2,0:T(8,128)(2,1)}, ...), condition=%wide.region_5.6_spmd.clone, body=%wide.region_2.5_spmd.clone.sunk | while | flops 868317696 | bytes 61567260 | solution.py:153
  62.1 4.5 fusion.134
  66.5 4.7 fusion.135
  82.1 4.5 fusion.134
  86.5 4.7 fusion.135
  102.1 4.5 fusion.134
  106.5 4.7 fusion.135
  122.0 4.5 fusion.134
  126.5 4.7 fusion.135
  139.9 36.2 %reduce-scatter.11.cloned.1.call-done = bf16[512,768]{1,0:T(8,128)(2,1)} async-done(((bf16[2048,768]{1,0:T(8,128)(2,1)}), bf16[512,768]{1,0:T(8,128)(2,1)}) %reduce-scatter.11.cloned.1.call-update) | async-done | bytes 786448 | tf_op jit(solution)/shard_map/reduce_scatter | solution.py:155
  183.7 28.0 %all-gather.6.cloned.1.call-done = bf16[2048,768]{1,0:T(8,128)(2,1)} async-done(((bf16[512,768]{1,0:T(8,128)(2,1)}), bf16[2048,768]{1,0:T(8,128)(2,1)}) %all-gather.6.cloned.1.call-update) | async-done | bytes 3145744 | tf_op jit(solution)/shard_map/all_gather | solution.py:163
  211.7 7.5 fusion.76
  219.2 22.5 %all-gather.8.cloned.1.call-done = bf16[2048,768]{1,0:T(8,128)(2,1)} async-done(((bf16[512,768]{1,0:T(8,128)(2,1)}), bf16[2048,768]{1,0:T(8,128)(2,1)}) %all-gather.8.cloned.1.call-update) | async-done | bytes 3145744 | tf_op jit(solution)/shard_map/all_gather | solution.py:175
  241.7 20.2 %convert_reduce_fusion = (f32[768]{0:T(1024)}, bf16[2048,768]{1,0:T(8,128)(2,1)S(1)}, f32[2048,768]{1,0:T(8,128)}) fusion(f32[2048,768]{1,0:T(8,128)} %fusion.76, f32[768]{0:T(1024)} %param.25, bf16[2048,768]{1,0:T(8,128)(2,1)} %all-gather.8.cloned.1.call-done, bf16[768,768]{1,0:T(8,128)(2,1)S(1)} %copy-done), kind=kOutput, calls=%fused_computation.44 | convolution fusion | flops 2533883136 | bytes 20060160 | tf_op jit(solution)/shard_map/td,fd->tf/dot_general | solution.py:179
  263.5 4.0 convolution_convert_fusion
  267.6 5.5 multiply_convert_fusion.1
  274.8 4.0 convolution_convert_fusion.1
  279.1 26.5 %reduce-scatter.15.cloned.1.call-done = bf16[512,768]{1,0:T(8,128)(2,1)} async-done(((bf16[2048,768]{1,0:T(8,128)(2,1)}), bf16[512,768]{1,0:T(8,128)(2,1)}) %reduce-scatter.15.cloned.1.call-update) | async-done | bytes 786448 | tf_op jit(solution)/shard_map/reduce_scatter | solution.py:184
  308.3 37.6 %reduce-scatter.13.cloned.1.call-done = bf16[512,768]{1,0:T(8,128)(2,1)} async-done(((bf16[2048,768]{1,0:T(8,128)(2,1)}), bf16[512,768]{1,0:T(8,128)(2,1)}) %reduce-scatter.13.cloned.1.call-update) | async-done | bytes 786448 | tf_op jit(solution)/shard_map/reduce_scatter | solution.py:166
  353.2 17.5 %collective-permute-done = bf16[512,768]{1,0:T(8,128)(2,1)S(1)} collective-permute-done((bf16[512,768]{1,0:T(8,128)(2,1)S(1)}, bf16[512,768]{1,0:T(8,128)(2,1)S(1)}, u32[]{:S(2)}, u32[]{:S(2)}) %collective-permute-start) | collective-permute-done | bytes 786464 | tf_op jit(solution)/shard_map/ppermute | solution.py:31
  370.7 11.5 %collective-permute-done.1 = bf16[512,768]{1,0:T(8,128)(2,1)} collective-permute-done((bf16[512,768]{1,0:T(8,128)(2,1)S(1)}, bf16[512,768]{1,0:T(8,128)(2,1)}, u32[]{:S(2)}, u32[]{:S(2)}) %collective-permute-start.1) | collective-permute-done | bytes 786464 | tf_op jit(solution)/shard_map/ppermute | solution.py:31
  385.1 4.4 gather_fusion
  389.5 4.2 convolution_bitcast_fusion
  393.7 4.0 convolution_convert_fusion.3
  398.7 141.7 %while.29 = (s32[]{:T(128)}, f32[2048,3,64]{0,2,1:T(8,128)}, f32[2048,3,64]{0,2,1:T(8,128)}, bf16[4,512,192]{1,2,0:T(8,128)(2,1)}, s32[4]{0:T(128)S(1)}, /*index...) while((s32[]{:T(128)}, f32[2048,3,64]{0,2,1:T(8,128)}, ...), condition=%wide.region_15.16_spmd.clone, body=%wide.region_13.15_spmd.clone.sunk | while | flops 2056321536 | bytes 143663600 | solution.py:241
  408.9 8.7 %multiply_reduce_fusion.4 = (f32[3,512]{1,0:T(4,128)S(1)}, f32[3,512,2048]{2,1,0:T(8,128)}) fusion(f32[3,512,2048]{2,1,0:T(8,128)S(1)} %fusion.146, f32[3,512]{1,0:T(4,128)S(1)} %dynamic-slice_bitcast_fusion.2, f32[512,2048]{1,0:T(8,128)S(1)} %add_sqrt_fusion.5, f32[3]{0:T(128)S(1)} %multiply_exponential_fusion.5, ...), kind=kOutput, calls=%fused_computation.19.clone.1 | convolution fusion | flops 424671744 | bytes 31404044 | tf_op jit(solution)/shard_map/while/body/eval_jaxpr/qhe,khe->hqk/dot_general | solution.py:122
  417.6 5.6 multiply_convert_fusion.4
  423.2 6.2 fusion.148
  444.3 8.7 %multiply_reduce_fusion.4 = (f32[3,512]{1,0:T(4,128)S(1)}, f32[3,512,2048]{2,1,0:T(8,128)}) fusion(f32[3,512,2048]{2,1,0:T(8,128)S(1)} %fusion.146, f32[3,512]{1,0:T(4,128)S(1)} %dynamic-slice_bitcast_fusion.2, f32[512,2048]{1,0:T(8,128)S(1)} %add_sqrt_fusion.5, f32[3]{0:T(128)S(1)} %multiply_exponential_fusion.5, ...), kind=kOutput, calls=%fused_computation.19.clone.1 | convolution fusion | flops 424671744 | bytes 31404044 | tf_op jit(solution)/shard_map/while/body/eval_jaxpr/qhe,khe->hqk/dot_general | solution.py:122
  453.0 5.6 multiply_convert_fusion.4
  458.6 6.1 fusion.148
  479.7 8.7 %multiply_reduce_fusion.4 = (f32[3,512]{1,0:T(4,128)S(1)}, f32[3,512,2048]{2,1,0:T(8,128)}) fusion(f32[3,512,2048]{2,1,0:T(8,128)S(1)} %fusion.146, f32[3,512]{1,0:T(4,128)S(1)} %dynamic-slice_bitcast_fusion.2, f32[512,2048]{1,0:T(8,128)S(1)} %add_sqrt_fusion.5, f32[3]{0:T(128)S(1)} %multiply_exponential_fusion.5, ...), kind=kOutput, calls=%fused_computation.19.clone.1 | convolution fusion | flops 424671744 | bytes 31404044 | tf_op jit(solution)/shard_map/while/body/eval_jaxpr/qhe,khe->hqk/dot_general | solution.py:122
  488.4 5.6 multiply_convert_fusion.4
  494.0 6.1 fusion.148
  515.0 8.7 %multiply_reduce_fusion.4 = (f32[3,512]{1,0:T(4,128)S(1)}, f32[3,512,2048]{2,1,0:T(8,128)}) fusion(f32[3,512,2048]{2,1,0:T(8,128)S(1)} %fusion.146, f32[3,512]{1,0:T(4,128)S(1)} %dynamic-slice_bitcast_fusion.2, f32[512,2048]{1,0:T(8,128)S(1)} %add_sqrt_fusion.5, f32[3]{0:T(128)S(1)} %multiply_exponential_fusion.5, ...), kind=kOutput, calls=%fused_computation.19.clone.1 | convolution fusion | flops 424671744 | bytes 31404044 | tf_op jit(solution)/shard_map/while/body/eval_jaxpr/qhe,khe->hqk/dot_general | solution.py:122
  523.7 5.6 multiply_convert_fusion.4
  529.3 6.1 fusion.148
  546.9 5.7 bitcast_convert_fusion
  552.7 7.0 fusion.78
  559.8 7.7 fusion.77
  567.9 5.9 fusion.32
  583.3 7.2 reduce-scatter.17.cloned.1.call-done
  596.9 41.8 %all-reduce = (f32[2,768]{1,0:T(2,128)}, f32[2,768]{1,0:T(2,128)}, f32[2,768]{1,0:T(2,128)}, f32[2,768]{1,0:T(2,128)}, f32[3072]{0:T(1024)}) all-reduce(f32[2,768]{1,0:T(2,128)} %pad_maximum_fusion.4, f32[2,768]{1,0:T(2,128)} %pad_maximum_fusion.5, ...), channel_id=1, replica_groups=mesh['dp'=8,'tensor'=4] {'dp','tensor'}, use_global_device_ids=true, to_apply=%region_21.22 | all-reduce | flops 9216 | bytes 73728 | tf_op jit(solution)/shard_map/psum | solution.py:274
  642.4 22.2 %reduce-scatter.23.cloned.1.call-done = f32[768,96]{0,1:T(8,128)} async-done(((f32[768,768]{0,1:T(8,128)}), f32[768,96]{0,1:T(8,128)}) %reduce-scatter.23.cloned.1.call-update) | async-done | bytes 294928 | tf_op jit(solution)/shard_map/reduce_scatter | solution.py:288
  664.5 72.7 %reduce-scatter.21.cloned.1.call-done = f32[96,768]{1,0:T(8,128)} async-done(((f32[768,768]{1,0:T(8,128)}), f32[96,768]{1,0:T(8,128)}) %reduce-scatter.21.cloned.1.call-update) | async-done | bytes 294928 | tf_op jit(solution)/shard_map/reduce_scatter | solution.py:287
  737.3 72.9 %reduce-scatter.19.cloned.1.call-done = f32[96,3,192]{2,0,1:T(8,128)} async-done(((f32[768,3,192]{2,0,1:T(8,128)}), f32[96,3,192]{2,0,1:T(8,128)}) %reduce-scatter.19.cloned.1.call-update) | async-done | bytes 221200 | tf_op jit(solution)/shard_map/reduce_scatter | solution.py:285
  (329 shorter events, 160.5 us)
Async XLA Ops:
  7.2 234.5 %copy-start = (bf16[768,768]{1,0:T(8,128)(2,1)S(1)}, bf16[768,768]{1,0:T(8,128)(2,1)}, u32[]{:S(2)}) copy-start(bf16[768,768]{1,0:T(8,128)(2,1)} %param.26) | copy-start | bytes 3538948
  7.2 7.5 copy-start.51
  7.2 8.2 %copy-start.50 = (s32[1,3]{1,0:T(1,128)S(1)}, s32[1,3]{1,0:T(1,128)}, u32[]{:S(2)}) copy-start(s32[1,3]{1,0:T(1,128)} %param.17) | copy-start | bytes 40
  7.2 38.8 %copy-start.53 = (bf16[768,3,192]{0,2,1:T(8,128)(2,1)S(1)}, bf16[768,3,192]{0,2,1:T(8,128)(2,1)}, u32[]{:S(2)}) copy-start(bf16[768,3,192]{0,2,1:T(8,128)(2,1)} %param.20) | copy-start | bytes 2654212
  7.2 38.8 %all-gather.4.cloned.1.call-start = ((), (), s32[]{:S(2)}) async-start(), calls=%async_computation.8 | async-start | bytes 3932160 | tf_op jit(solution)/shard_map/all_gather | solution.py:109
  8.7 41.2 %copy-start.30 = (f32[512]{0:T(512)}, f32[512]{0:T(512)S(1)}, u32[]{:S(2)}) copy-start(f32[512]{0:T(512)S(1)} %broadcast_multiply_fusion.1) | copy-start | bytes 6148
  10.8 39.1 %copy-start.36 = (f32[512]{0:T(512)}, f32[512]{0:T(512)S(1)}, u32[]{:S(2)}) copy-start(f32[512]{0:T(512)S(1)} %fusion.65) | copy-start | bytes 6148
  12.2 37.7 %copy-start.26 = (f32[768]{0:T(1024)}, f32[768]{0:T(1024)S(1)}, u32[]{:S(2)}) copy-start(f32[768]{0:T(1024)S(1)} %get-tuple-element.314) | copy-start | bytes 9220
  14.6 161.5 %reduce-scatter.11.cloned.1.call-start = ((), (), s32[]{:S(2)}) async-start(), calls=%async_computation.9 | async-start | bytes 3932160 | tf_op jit(solution)/shard_map/reduce_scatter | solution.py:155
  132.6 5.5 copy-start.14
  138.0 38.1 %copy-start.2 = (bf16[512,768]{1,0:T(8,128)(2,1)S(1)}, bf16[512,768]{1,0:T(8,128)(2,1)}, u32[]{:S(2)}) copy-start(bf16[512,768]{1,0:T(8,128)(2,1)} %param.16) | copy-start | bytes 2359300
  138.1 73.7 %all-gather.6.cloned.1.call-start = ((), (), s32[]{:S(2)}) async-start(), calls=%async_computation.10 | async-start | bytes 3932160 | tf_op jit(solution)/shard_map/all_gather | solution.py:163
  183.1 58.6 %all-gather.8.cloned.1.call-start = ((), (), s32[]{:S(2)}) async-start(), calls=%async_computation.12 | async-start | bytes 3932160 | tf_op jit(solution)/shard_map/all_gather | solution.py:175
  183.6 121.9 %reduce-scatter.15.cloned.1.call-start = ((), (), s32[]{:S(2)}) async-start(), calls=%async_computation.13 | async-start | bytes 3932160 | tf_op jit(solution)/shard_map/reduce_scatter | solution.py:184
  241.7 21.8 %copy-start.52 = (bf16[768,768]{1,0:T(8,128)(2,1)S(1)}, bf16[768,768]{1,0:T(8,128)(2,1)}, u32[]{:S(2)}) copy-start(bf16[768,768]{1,0:T(8,128)(2,1)} %param.24) | copy-start | bytes 3538948
  267.5 78.3 %reduce-scatter.13.cloned.1.call-start = ((), (), s32[]{:S(2)}) async-start(), calls=%async_computation.11 | async-start | bytes 3932160 | tf_op jit(solution)/shard_map/reduce_scatter | solution.py:166
  278.8 26.8 %copy-start.25 = (f32[768]{0:T(1024)S(1)}, f32[768]{0:T(1024)}, u32[]{:S(2)}) copy-start(f32[768]{0:T(1024)} %get-tuple-element.231) | copy-start | bytes 9220
  278.8 26.8 %copy-start.29 = (f32[512]{0:T(512)S(1)}, f32[512]{0:T(512)}, u32[]{:S(2)}) copy-start(f32[512]{0:T(512)} %dynamic-slice_convert_fusion) | copy-start | bytes 6148
  278.8 26.8 %copy-start.32 = (f32[768]{0:T(1024)S(1)}, f32[768]{0:T(1024)}, u32[]{:S(2)}) copy-start(f32[768]{0:T(1024)} %get-tuple-element.313) | copy-start | bytes 9220
  278.8 26.8 %copy-start.34 = (f32[512]{0:T(512)S(1)}, f32[512]{0:T(512)}, u32[]{:S(2)}) copy-start(f32[512]{0:T(512)} %copy-done.33) | copy-start | bytes 6148
  278.8 26.8 %copy-start.39 = (f32[512]{0:T(512)S(1)}, f32[512]{0:T(512)}, u32[]{:S(2)}) copy-start(f32[512]{0:T(512)} %copy-done.38) | copy-start | bytes 6148
  278.8 29.5 %copy-start.43 = (f32[512]{0:T(512)S(1)}, f32[512]{0:T(512)}, u32[]{:S(2)}) copy-start(f32[512]{0:T(512)} %copy-done.42) | copy-start | bytes 6148
  278.8 67.0 %copy-start.45 = (f32[768]{0:T(1024)S(1)}, f32[768]{0:T(1024)}, u32[]{:S(2)}) copy-start(f32[768]{0:T(1024)} %get-tuple-element.230) | copy-start | bytes 9220
  278.9 302.8 %reduce-scatter.25.cloned.1.call-start = ((), (), s32[]{:S(2)}) async-start(), calls=%async_computation.18 | async-start | bytes 884736
  308.3 42.1 %copy-start.15 = (bf16[512,768]{1,0:T(8,128)(2,1)S(1)}, bf16[512,768]{1,0:T(8,128)(2,1)}, u32[]{:S(2)}) copy-start(bf16[512,768]{1,0:T(8,128)(2,1)} %param.27) | copy-start | bytes 2359300
  349.2 35.9 %copy-start.40 = (f32[512]{0:T(512)}, f32[512]{0:T(512)S(1)}, u32[]{:S(2)}) copy-start(f32[512]{0:T(512)S(1)} %negate_multiply_fusion.2) | copy-start | bytes 6148
  351.5 19.2 %collective-permute-start = (bf16[512,768]{1,0:T(8,128)(2,1)S(1)}, bf16[512,768]{1,0:T(8,128)(2,1)S(1)}, u32[]{:S(2)}, u32[]{:S(2)}) collective-permute-start(bf16[512,768]{1,0:T(8,128)(2,1)S(1)} %get-tuple-element.302), channel_id=1, source_target_pairs={{0,1},{1,2},{2,3},{3,0},{4,5},{5,6},{6,7},{7,4},{8,9},{9,10},{10,1... | collective-permute-start | bytes 2359304 | tf_op jit(solution)/shard_map/ppermute | solution.py:31
  351.5 19.2 %collective-permute-start.2 = (bf16[512,768]{1,0:T(8,128)(2,1)S(1)}, bf16[512,768]{1,0:T(8,128)(2,1)S(1)}, u32[]{:S(2)}, u32[]{:S(2)}) collective-permute-start(bf16[512,768]{1,0:T(8,128)(2,1)S(1)} %get-tuple-element.302), channel_id=1, source_target_pairs={{1,0},{2,1},{3,2},{0,3},{5,4},{6,5},{7,6},{4,7},{9,8},{10,9},{11,1... | collective-permute-start | bytes 2359304 | tf_op jit(solution)/shard_map/ppermute | solution.py:33
  370.7 11.5 %collective-permute-start.1 = (bf16[512,768]{1,0:T(8,128)(2,1)S(1)}, bf16[512,768]{1,0:T(8,128)(2,1)}, u32[]{:S(2)}, u32[]{:S(2)}) collective-permute-start(bf16[512,768]{1,0:T(8,128)(2,1)S(1)} %collective-permute-done), channel_id=1, source_target_pairs={{0,1},{1,2},{2,3},{3,0},{4,5},{5,6},{6,7},{7,4},{8,9},{9,10},{10,1... | collective-permute-start | bytes 2359304 | tf_op jit(solution)/shard_map/ppermute | solution.py:31
  393.7 196.8 %reduce-scatter.17.cloned.1.call-start = ((), (), s32[]{:S(2)}) async-start(), calls=%async_computation.14 | async-start | bytes 3932160 | tf_op jit(solution)/shard_map/reduce_scatter | solution.py:257
  417.6 5.6 copy-start.6
  453.0 5.6 copy-start.6
  488.4 5.6 copy-start.6
  523.7 5.6 copy-start.6
  552.7 111.9 %reduce-scatter.23.cloned.1.call-start = ((), (), s32[]{:S(2)}) async-start(), calls=%async_computation.17 | async-start | bytes 2654208 | tf_op jit(solution)/shard_map/reduce_scatter | solution.py:288
  559.7 8.1 copy-start.20
  559.7 8.1 copy-start.22
  559.7 177.5 %reduce-scatter.21.cloned.1.call-start = ((), (), s32[]{:S(2)}) async-start(), calls=%async_computation.16 | async-start | bytes 2654208 | tf_op jit(solution)/shard_map/reduce_scatter | solution.py:287
  567.5 8.7 %copy-start.44 = (f32[768]{0:T(1024)S(1)}, f32[768]{0:T(1024)}, u32[]{:S(2)}) copy-start(f32[768]{0:T(1024)} %get-tuple-element.229) | copy-start | bytes 9220
  567.5 12.0 %copy-start.16 = (bf16[4,512,192]{1,2,0:T(8,128)(2,1)S(1)}, bf16[4,512,192]{1,2,0:T(8,128)(2,1)}, u32[]{:S(2)}) copy-start(bf16[4,512,192]{1,2,0:T(8,128)(2,1)} %get-tuple-element.145) | copy-start | bytes 2359300
  567.6 242.6 %reduce-scatter.19.cloned.1.call-start = ((), (), s32[]{:S(2)}) async-start(), calls=%async_computation.15 | async-start | bytes 2654208 | tf_op jit(solution)/shard_map/reduce_scatter | solution.py:285
  573.8 16.7 %copy-start.3 = (bf16[512,768]{1,0:T(8,128)(2,1)S(1)}, bf16[512,768]{1,0:T(8,128)(2,1)}, u32[]{:S(2)}) copy-start(bf16[512,768]{1,0:T(8,128)(2,1)} %param.16) | copy-start | bytes 2359300
  573.8 16.7 %copy-start.27 = (f32[768]{0:T(1024)S(1)}, f32[768]{0:T(1024)}, u32[]{:S(2)}) copy-start(f32[768]{0:T(1024)} %copy-done.26) | copy-start | bytes 9220
  573.8 16.7 %copy-start.31 = (f32[512]{0:T(512)S(1)}, f32[512]{0:T(512)}, u32[]{:S(2)}) copy-start(f32[512]{0:T(512)} %copy-done.30) | copy-start | bytes 6148
  573.8 19.2 %copy-start.37 = (f32[512]{0:T(512)S(1)}, f32[512]{0:T(512)}, u32[]{:S(2)}) copy-start(f32[512]{0:T(512)} %copy-done.36) | copy-start | bytes 6148
  573.8 65.6 %copy-start.13 = (f32[512,768]{1,0:T(8,128)S(1)}, f32[512,768]{1,0:T(8,128)}, u32[]{:S(2)}) copy-start(f32[512,768]{1,0:T(8,128)} %copy-done.12) | copy-start | bytes 4718596
  590.5 5.8 copy-start.46
  592.2 217.9 %copy-start.1 = (bf16[768,768]{1,0:T(8,128)(2,1)S(1)}, bf16[768,768]{1,0:T(8,128)(2,1)}, u32[]{:S(2)}) copy-start(bf16[768,768]{1,0:T(8,128)(2,1)} %param.26) | copy-start | bytes 3538948
  (36 other events, 97.3 us)
Sparse Core Ops, SparseCore 0:
  14.8 31.2 all-gather.3
  138.2 37.8 reduce-scatter.10
  183.2 28.4 all-gather.5
  213.1 28.4 all-gather.7
  267.7 37.8 reduce-scatter.14
  308.0 37.8 reduce-scatter.12
  393.8 63.0 reduce-scatter.24
  552.8 37.6 reduce-scatter.16
  594.6 69.9 reduce-scatter.22
  668.5 68.7 reduce-scatter.20
  741.3 68.7 reduce-scatter.18
